TPU v7x, 256 devices: a whole 4x4x8 slice. The times are simulated.
256 devices in a mesh: leaf: 64 (over z, y, core), blk: 4 (over x).
Axes of the slice: x: 4, y: 4, z: 8, core: 2. Of those that a mesh axis runs over, the one named last changes fastest.
Arguments:
- src_pos: int32 [4, 16777216], P('blk', 'leaf'), may hold values from 0 to 67108863, as said below
- strengths: float32 [2, 4, 16777216], P(None, 'blk', 'leaf'), may hold values from -0.0007324219 to 0.0007324219
- tgt_pos: int32 [67108864], P(('leaf', 'blk')), may hold values from 0 to 201326591, as said below
Outputs:
- field: float32 [2, 67108864], P(None, ('leaf', 'blk'))
Inputs may be any that keep to these rules, and one draw needn't show every extreme that they name: `src_pos`: row q holds 131072 runs of 128 cells; run b lies in the 128 cells from (q * 131072 + b) * 128 on. `tgt_pos`: the ticks held by index k of leaf, at every index of blk, come in 2048 runs of 128; run j lies in the 1536 ticks from (j * 64 + r) * 1536 on, where r is k with its 6 binary digits in reverse order.
All inputs are finite; a program needn't handle non-finite values.
Results may differ from a plain program's by a relative error of at most 0.0003.
Values sent between devices are 32-bit elements; how exact they have to be, the bound alone decides.
A program may use at most 128 MiB of HBM per device.

v0:
```python
import functools
import math

import jax
import jax.numpy as jnp
import numpy as np
from jax import lax
from jax.experimental import pallas as pl
from jax.experimental.pallas import tpu as pltpu
from jax.sharding import PartitionSpec as P

R = 16
CELLS = 128
TOP_TICKS = 201326592
BOX_TICKS = 1536
HALF = BOX_TICKS // 2
N_BLK = 4
MESH = pl.DeviceIdType.MESH


def node_offsets(box_cells):
    unit = (1.0 - np.cos(np.pi * (np.arange(R) + 0.5) / R)) / 2.0
    return np.floor(box_cells * unit).astype(np.int64)


def lagrange_values(node_pos, points):
    rows = []
    for a in range(node_pos.shape[0]):
        col = np.ones(points.shape[0])
        for b in range(node_pos.shape[0]):
            if b != a:
                col = col * (points - node_pos[b]) / (node_pos[a] - node_pos[b])
        rows.append(col)
    return np.stack(rows)


def phase(ticks, cells):
    product = (int(ticks) * np.asarray(cells, np.int64)) % (1 << 32)
    return np.exp(2j * np.pi * product / 2.0**32)


def level_matrix(level):
    cells = CELLS << level
    child, parent = node_offsets(cells), node_offsets(2 * cells)
    inner = np.concatenate([child, child + cells])
    blend = lagrange_values(parent / (2.0 * cells), inner / (2.0 * cells))
    blend = blend.astype(np.float32).astype(np.float64).reshape(R, 2, R)
    signed = blend * np.array([1.0, -1.0])[None, :, None]
    quarter = (TOP_TICKS >> level) // 4
    sides = [phase(-quarter, child), phase(quarter, child)]
    return np.stack([signed * side[None, None, :] for side in sides])


def stage_complex(first, count):
    out = np.eye(R, dtype=np.complex128).reshape(1, R, 1, R)
    for level in range(first, first + count):
        step = level_matrix(level)
        joined = np.einsum("etju,aubs->aetjbs", step, out)
        n = out.shape[0]
        out = joined.reshape(2 * n, R, 2 * n, R)
    return out


def real_form(mat):
    n, m = mat.shape[0], mat.shape[2]
    out = np.zeros((n, 2, R, m, 2, R))
    out[:, 0, :, :, 0] = mat.real
    out[:, 0, :, :, 1] = -mat.imag
    out[:, 1, :, :, 0] = mat.imag
    out[:, 1, :, :, 1] = mat.real
    return out.reshape(n * 2 * R, m * 2 * R)


def leaf_map():
    nodes = node_offsets(CELLS)
    angles = np.pi * (np.arange(R) + 0.5) / R
    at_exact = lagrange_values(2.0 * nodes / CELLS - 1.0, np.cos(angles))
    cheb = np.stack([np.cos(n * angles) for n in range(R)])
    norm = np.where(np.arange(R) == 0, 1.0, 2.0) / R
    coef = (norm[:, None] * (cheb @ at_exact.T)).astype(np.float32).astype(np.float64)
    split = np.zeros((R, R))
    for n in range(8):
        split[n, n] = 1.0
    split[8, 8] = 1.0
    for i in range(1, 8):
        split[8 + i, 8 + i] = 2.0
        split[8 + i, 8 - i] -= 1.0
    return coef.T @ split


def stage_tables():
    mats = []
    leaf = leaf_map()
    first = stage_complex(0, 3)
    mats.append(real_form(np.einsum("atbs,sn->atbn", first, leaf)))
    mats.append(real_form(stage_complex(3, 3)))
    mats.append(real_form(stage_complex(6, 3)))
    two = stage_complex(9, 2)
    wide = np.einsum("atbs,ij->aitbjs", two, np.eye(2)).reshape(8, R, 8, R)
    mats.append(real_form(wide))
    mats.append(real_form(stage_complex(11, 3)))
    mats.append(real_form(stage_complex(14, 3)))
    return np.stack(mats)


def top_frequency():
    nodes = node_offsets(CELLS << 17)
    q = np.arange(N_BLK)[:, None]
    return nodes, nodes[None, :] / 2.0**32 + q / 256.0


def hi_lo(table):
    full = np.asarray(table, np.float32)
    hi = full.astype(jnp.bfloat16)
    lo = (full - hi.astype(np.float32)).astype(jnp.bfloat16)
    return hi, lo


@functools.lru_cache(None)
def tables():
    hi, lo = hi_lo(stage_tables())
    stages = np.stack([hi, lo], axis=1)
    nodes, freq = top_frequency()
    y = np.arange(HALF) + 0.5
    angle = 2.0 * np.pi * ((freq.reshape(-1)[:, None] * y[None, :]) % 1.0)
    wave_hi, wave_lo = hi_lo(np.concatenate([np.cos(angle), np.sin(angle)], axis=1))
    waves = np.concatenate([wave_hi, wave_hi, wave_lo, wave_lo], axis=0)
    q = np.arange(N_BLK)[:, None]
    shift = np.exp(2j * np.pi * ((-0.5 * nodes[None, :] / 2.0**32 + q * (HALF - 0.5) / 256.0) % 1.0))
    shift = np.concatenate([shift.real, shift.imag], axis=1).astype(np.float32)
    shift = np.broadcast_to(shift[:, :, None], (N_BLK, 2 * R, 128)).copy()
    turns = (3 * np.arange(CELLS)) % CELLS / CELLS
    spin = np.stack([np.cos(2 * np.pi * turns), np.sin(2 * np.pi * turns)]).astype(np.float32)
    spin = np.broadcast_to(spin[:, None, :], (2, 8, CELLS)).copy()
    return stages, waves, shift, spin


def swap_lane(blocks, row_bit, lane_bit):
    out = list(blocks)
    amount = 1 << lane_bit
    for i in range(len(blocks)):
        if i >> row_bit & 1:
            continue
        k = i | 1 << row_bit
        x0, x1 = blocks[i], blocks[k]
        mask = (lax.broadcasted_iota(jnp.int32, x0.shape, 1) & amount) != 0
        out[i] = jnp.where(mask, pltpu.roll(x1, amount, 1), x0)
        out[k] = jnp.where(mask, x1, pltpu.roll(x0, 128 - amount, 1))
    return out


def swap_half(left, right, row_bit):
    left, right = list(left), list(right)
    for i in range(len(left)):
        if i >> row_bit & 1:
            continue
        k = i | 1 << row_bit
        left[k], right[i] = right[i], left[k]
    return left, right


def gather_rows(blocks):
    return jnp.concatenate(blocks, axis=0)


def split_rows(x, rows):
    return [x[i * rows : (i + 1) * rows] for i in range(x.shape[0] // rows)]


def apply_stage(stage_ref, index, left, right):
    x = jnp.concatenate([left, right], axis=1)
    hi = x.astype(jnp.bfloat16)
    lo = (x - hi.astype(jnp.float32)).astype(jnp.bfloat16)
    w_hi, w_lo = stage_ref[index, 0], stage_ref[index, 1]
    dot = functools.partial(jnp.dot, preferred_element_type=jnp.float32)
    y = dot(w_hi, hi) + (dot(w_lo, hi) + dot(w_hi, lo))
    return y[:, :128], y[:, 128:]


LAG = 2


def leaf_sums(pos, amp, spin_re, spin_im, mom, half):
    def beta_step(beta, carry):
        cells, amp_re, amp_im = [], [], []
        for group in range(16):
            s7, s6, s10, s9 = group >> 3 & 1, group >> 2 & 1, group >> 1 & 1, group & 1
            slab, rows = s10 * 2 + s9, pl.ds(beta + s6 * 64 + s7 * 128, 8, stride=8)
            cell = pos[slab, half, rows, :] & (CELLS - 1)
            sr, si = amp[0, slab, half, rows, :], amp[1, slab, half, rows, :]
            wr = jnp.take_along_axis(spin_re, cell, axis=1)
            wi = jnp.take_along_axis(spin_im, cell, axis=1)
            cells.append(cell.astype(jnp.float32) * (2.0 / CELLS) - 1.0)
            amp_re.append(wr * sr - wi * si)
            amp_im.append(wi * sr + wr * si)
        v_all = jnp.concatenate(cells, axis=0).T
        re_all = jnp.concatenate(amp_re, axis=0).T
        im_all = jnp.concatenate(amp_im, axis=0).T
        acc = [None] * 32
        for step in range(16):
            rows = slice(step * 8, step * 8 + 8)
            v, sr, si = v_all[rows], re_all[rows], im_all[rows]
            cheb = [None, v]
            twice = v + v
            cheb.append(twice * v - 1.0)
            for n in range(3, 9):
                cheb.append(twice * cheb[-1] - cheb[-2])
            for side, (a, b) in enumerate(((sr, si), (cheb[8] * sr, cheb[8] * si))):
                for n in range(8):
                    pa = a if n == 0 else cheb[n] * a
                    pb = b if n == 0 else cheb[n] * b
                    ia, ib = side * 8 + n, 16 + side * 8 + n
                    acc[ia] = pa if acc[ia] is None else acc[ia] + pa
                    acc[ib] = pb if acc[ib] is None else acc[ib] + pb
        for n in range(32):
            mom[beta, n : n + 1, half * 128 : half * 128 + 128] = jnp.sum(acc[n], axis=0, keepdims=True)
        return carry

    lax.fori_loop(0, 8, beta_step, 0)


def lane_swaps(x, pairs):
    blocks = split_rows(x, 32)
    for row_bit, lane_bit in pairs:
        blocks = swap_lane(blocks, row_bit, lane_bit)
    return blocks


def local_tree(stage, mom, out):
    sums = mom[...].reshape(256, 256)
    left, right = apply_stage(stage, 0, sums[:, :128], sums[:, 128:])
    pairs = ((2, 2), (1, 1), (0, 0))
    left, right = apply_stage(
        stage, 1, gather_rows(lane_swaps(left, pairs)), gather_rows(lane_swaps(right, pairs))
    )
    pairs = ((1, 6), (0, 5))
    left, right = swap_half(lane_swaps(left, pairs), lane_swaps(right, pairs), 2)
    left, right = apply_stage(stage, 2, gather_rows(left), gather_rows(right))
    pairs = ((2, 4), (1, 3), (0, 2))
    left, right = apply_stage(
        stage, 3, gather_rows(lane_swaps(left, pairs)), gather_rows(lane_swaps(right, pairs))
    )
    for half, x in enumerate((left, right)):
        tiles = split_rows(x, 8)
        tiles = swap_lane(swap_lane(tiles, 1, 1), 0, 0)
        for i in range(32):
            e9, e10, e0, e1, e2 = i >> 4 & 1, i >> 3 & 1, i >> 2 & 1, i >> 1 & 1, i & 1
            out[e0 * 32 + e1 * 16 + e2 * 8 + e9 * 4 + e10 * 2 + half] = tiles[i]


def cross_tree(stage, shift, got, out):
    halves = []
    for half in range(2):
        tiles = [None] * 32
        for d in range(32):
            tiles[(d & 7) * 4 + (d >> 4 & 1) * 2 + (d >> 3 & 1)] = got[half * 32 + d]
        halves.append(swap_lane(swap_lane(tiles, 1, 1), 0, 0))
    left, right = apply_stage(stage, 4, gather_rows(halves[0]), gather_rows(halves[1]))
    pairs = ((1, 1), (0, 0))
    left, right = swap_half(lane_swaps(left, pairs), lane_swaps(right, pairs), 2)
    left, right = apply_stage(stage, 5, gather_rows(left), gather_rows(right))
    shift_re, shift_im = shift[:R], shift[R:]
    for half, x in enumerate((left, right)):
        turned = []
        for block in split_rows(x, 32):
            re, im = block[:R], block[R:]
            turned.append(shift_re * re - shift_im * im)
            turned.append(shift_im * re + shift_re * im)
        tiles = split_rows(gather_rows(turned), 8)
        tiles = swap_lane(swap_lane(tiles, 1, 1), 0, 0)
        for i in range(32):
            e14, e15, e16, e12, e13 = i >> 4 & 1, i >> 3 & 1, i >> 2 & 1, i >> 1 & 1, i & 1
            out[half + e12 * 2 + e13 * 4 + e14 * 8 + e15 * 16 + e16 * 32] = tiles[i]


def coefficients(roots, z):
    parts = [[], []]
    for q in range(N_BLK):
        for half in range(2):
            tiles = [roots[q, z * 8 + (c * 2 + half)] for c in range(4)]
            parts[half].append(swap_lane(swap_lane(tiles, 1, 1), 0, 0))
    out = []
    for half in range(2):
        sides = []
        for c in range(2):
            rows = []
            for q in range(N_BLK):
                rows += parts[half][q][2 * c : 2 * c + 2]
            x = jnp.concatenate(rows, axis=0)
            hi = x.astype(jnp.bfloat16).astype(jnp.float32)
            t = jnp.concatenate([hi, x - hi], axis=0).T.astype(jnp.bfloat16)
            sides.append(jnp.concatenate([t, t], axis=1))
        out.append(sides)
    return out


def look_up(dense, tick, out, z, half, reverse):
    sub = lax.broadcasted_iota(jnp.int32, (8, 128), 0)
    for i in range(16):
        row = i * 8
        base = z * 256 + (half * 128 + row)
        y = tick[pl.ds(base, 8), :] - ((base + sub) * 64 + reverse) * BOX_TICKS - HALF
        upper = y >= 0
        index = jnp.where(upper, y, -1 - y)
        low, high = index & 127, index >> 7
        sums = [None] * 4
        for h in range(6):
            pick = high == h
            for c in range(2):
                for part in range(2):
                    start = part * HALF + h * 128
                    got = jnp.take_along_axis(dense[c, row : row + 8, start : start + 128], low, axis=1)
                    k = c * 2 + part
                    sums[k] = got if h == 0 else jnp.where(pick, got, sums[k])
        re_even, re_odd, im_even, im_odd = sums
        re_odd = jnp.where(upper, re_odd, -re_odd)
        im_odd = jnp.where(upper, im_odd, -im_odd)
        out[pl.ds(base * 2, 8, stride=2), :] = re_even - im_odd
        out[pl.ds(base * 2 + 1, 8, stride=2), :] = im_even + re_odd


def kernel(
    pos_in, amp_in, tick_in, stage_in, wave_in, shift_in, spin_in, out_hbm,
    pos, amp, tick, stage, wave, shift, spin, mom,
    first_src, first_dst, second_src, roots, out, dense0, dense1,
    load_sem, store_sem, send1, recv1, send2, recv2, send3, recv3,
):
    leaf, blk = lax.axis_index("leaf"), lax.axis_index("blk")
    own_z = leaf // 8

    loads = [
        pltpu.make_async_copy(spin_in, spin, load_sem.at[0]),
        pltpu.make_async_copy(pos_in.at[:, 0], pos.at[:, 0], load_sem.at[1]),
        pltpu.make_async_copy(amp_in.at[:, :, 0], amp.at[:, :, 0], load_sem.at[2]),
        pltpu.make_async_copy(pos_in.at[:, 1], pos.at[:, 1], load_sem.at[3]),
        pltpu.make_async_copy(amp_in.at[:, :, 1], amp.at[:, :, 1], load_sem.at[4]),
        pltpu.make_async_copy(stage_in, stage, load_sem.at[5]),
        pltpu.make_async_copy(shift_in.at[blk], shift, load_sem.at[6]),
        pltpu.make_async_copy(wave_in, wave, load_sem.at[7]),
        pltpu.make_async_copy(tick_in, tick, load_sem.at[8]),
    ]
    for load in loads:
        load.start()
    barrier = pltpu.get_barrier_semaphore()

    def greet(i, carry):
        pl.semaphore_signal(barrier, inc=1, device_id={"leaf": leaf ^ i}, device_id_type=MESH)
        return carry

    lax.fori_loop(1, 64, greet, 0)
    for i in range(1, N_BLK):
        pl.semaphore_signal(barrier, inc=1, device_id={"blk": (blk + i) % N_BLK}, device_id_type=MESH)

    for load in loads[:3]:
        load.wait()
    spin_re, spin_im = spin[0], spin[1]
    leaf_sums(pos, amp, spin_re, spin_im, mom, 0)
    for load in loads[3:5]:
        load.wait()
    leaf_sums(pos, amp, spin_re, spin_im, mom, 1)
    loads[5].wait()
    local_tree(stage, mom, first_src)
    pl.semaphore_wait(barrier, 63 + N_BLK - 1)

    def first(i):
        return pltpu.make_async_remote_copy(
            src_ref=first_src.at[leaf ^ i],
            dst_ref=first_dst.at[leaf],
            send_sem=send1.at[i],
            recv_sem=recv1.at[i],
            device_id={"leaf": leaf ^ i},
            device_id_type=MESH,
        )

    def first_send(i, carry):
        first(i).start()
        return carry

    def first_wait(i, carry):
        first(i).wait()
        return carry

    lax.fori_loop(1, 64, first_send, 0)
    first_dst[leaf] = first_src[leaf]
    loads[6].wait()
    lax.fori_loop(1, 64, first_wait, 0)
    cross_tree(stage, shift[...], first_dst, second_src)

    def near_z(c):
        k = (c + 1) // 2
        return (own_z + k * (2 * (c % 2) - 1) + 8) % 8

    def second(c, j):
        other = near_z(c) * 8 + j
        return pltpu.make_async_remote_copy(
            src_ref=second_src.at[other],
            dst_ref=roots.at[blk, leaf],
            send_sem=send2.at[other],
            recv_sem=recv2.at[leaf],
            device_id={"leaf": other},
            device_id_type=MESH,
        )

    def second_got(z, j):
        other = z * 8 + j
        return pltpu.make_async_remote_copy(
            src_ref=second_src.at[other],
            dst_ref=roots.at[blk, other],
            send_sem=send2.at[other],
            recv_sem=recv2.at[other],
            device_id={"leaf": other},
            device_id_type=MESH,
        )

    own_j = leaf % 8

    def send_own(i, carry):
        second(0, (own_j + i) % 8).start()
        return carry

    lax.fori_loop(1, 8, send_own, 0)

    def send_far(n, carry):
        second(n // 8, (own_j + n) % 8).start()
        return carry

    lax.fori_loop(8, 64, send_far, 0)
    roots[blk, leaf] = second_src[leaf]
    loads[7].wait()
    loads[8].wait()

    def third(z, i):
        return pltpu.make_async_remote_copy(
            src_ref=roots.at[blk, pl.ds(z * 8, 8)],
            dst_ref=roots.at[blk, pl.ds(z * 8, 8)],
            send_sem=send3.at[z, i],
            recv_sem=recv3.at[z, i],
            device_id={"blk": (blk + i) % N_BLK},
            device_id_type=MESH,
        )

    def third_got(z, i):
        source = (blk + N_BLK - i) % N_BLK
        return pltpu.make_async_remote_copy(
            src_ref=roots.at[blk, pl.ds(z * 8, 8)],
            dst_ref=roots.at[source, pl.ds(z * 8, 8)],
            send_sem=send3.at[z, i],
            recv_sem=recv3.at[z, i],
            device_id={"blk": (blk + i) % N_BLK},
            device_id_type=MESH,
        )

    def store(z):
        return pltpu.make_async_copy(
            out.at[pl.ds(z * 512, 512)], out_hbm.at[pl.ds(z * 512, 512)], store_sem.at[z]
        )

    reverse = jnp.int32(0)
    for bit in range(6):
        reverse = reverse * 2 + (leaf // 2**bit) % 2

    def chunk_step(c, carry):
        @pl.when(c < 8)
        def _():
            z = near_z(c)

            def got(j, carry):
                second_got(z, (own_j + j) % 8).wait_recv()
                return carry

            lax.fori_loop(jnp.where(c == 0, 1, 0), 8, got, 0)
            for i in (2, 1, 3):
                third(z, i).start()

        @pl.when(c >= LAG)
        def _():
            z = near_z(c - LAG)
            for i in (1, 2, 3):
                third_got(z, i).wait_recv()
            lhs = coefficients(roots, z)
            for half, dense in enumerate((dense0, dense1)):
                for side in range(2):
                    dense[side] = jnp.dot(lhs[half][side], wave[...], preferred_element_type=jnp.float32)
            for half, dense in enumerate((dense0, dense1)):
                look_up(dense, tick, out, z, half, reverse)
            store(z).start()

        return carry

    lax.fori_loop(0, 8 + LAG, chunk_step, 0)

    def finish(z, carry):
        store(z).wait()
        for i in (1, 2, 3):
            third(z, i).wait_send()
        return carry

    lax.fori_loop(0, 8, finish, 0)

    def finish_second(i, carry):
        second_got(0, leaf ^ i).wait_send()
        return carry

    lax.fori_loop(1, 64, finish_second, 0)


def local(src_pos, strengths, tgt_pos):
    stages, waves, shift, spin = tables()
    hbm = pl.BlockSpec(memory_space=pl.ANY)
    vmem, dma = pltpu.VMEM, pltpu.SemaphoreType.DMA
    f32, tiles = jnp.float32, (64, 8, 128)
    out = pl.pallas_call(
        kernel,
        out_shape=jax.ShapeDtypeStruct((4096, 128), f32),
        in_specs=[hbm] * 7,
        out_specs=hbm,
        scratch_shapes=[
            vmem((4, 2, 256, 128), jnp.int32),
            vmem((2, 4, 2, 256, 128), f32),
            vmem((2048, 128), jnp.int32),
            vmem((6, 2, 256, 256), jnp.bfloat16),
            vmem((256, 2 * HALF), jnp.bfloat16),
            vmem((2 * R, 128), f32),
            vmem((2, 8, 128), f32),
            vmem((8, 32, 256), f32),
            vmem(tiles, f32),
            vmem(tiles, f32),
            vmem(tiles, f32),
            vmem((N_BLK, *tiles), f32),
            vmem((4096, 128), f32),
            vmem((2, 128, 2 * HALF), f32),
            vmem((2, 128, 2 * HALF), f32),
            dma((9,)),
            dma((8,)),
            dma((64,)),
            dma((64,)),
            dma((64,)),
            dma((64,)),
            dma((8, N_BLK)),
            dma((8, N_BLK)),
        ],
        compiler_params=pltpu.CompilerParams(collective_id=0, has_side_effects=True),
        name="butterfly",
    )(
        src_pos.reshape(4, 2, 256, 128),
        strengths.reshape(2, 4, 2, 256, 128),
        tgt_pos.reshape(2048, 128),
        jnp.asarray(stages),
        jnp.asarray(waves),
        jnp.asarray(shift),
        jnp.asarray(spin),
    )
    return jnp.transpose(out.reshape(2048, 2, 128), (1, 0, 2)).reshape(2, 2048 * 128)


def solution(mesh):
    return jax.shard_map(
        local,
        mesh=mesh,
        in_specs=(P("blk", "leaf"), P(None, "blk", "leaf"), P(("leaf", "blk"))),
        out_specs=P(None, ("leaf", "blk")),
        check_vma=False,
    )
```

profile of v0, /device:TPU:1, one launch (start us, length us, event | category | flops | bytes accessed | tf_op | source)
XLA Modules:
  0.0 55.3 jit_solution(5707038713496557348)
XLA Ops:
  0.0 52.7 %butterfly.1 = f32[4096,128]{1,0:T(8,128)} custom-call(s32[4,2,256,128]{3,2,1,0:T(8,128)} %bitcast.10, f32[2,4,2,256,128]{4,3,2,1,0:T(8,128)} %bitcast.9, s32[2048,128]{1,0:T(8,128)} %bitcast.11, bf16[6,2,256,256]{3,2,1,0:T(8,128)(2,1)} %constant.8.clone.stage_in, bf16[256,1536]{1,0:T(8,128)(2,1)} %constant.9.clone.wave_in, ...), custom_call_target="tpu_custom_call" | custom-call | tf_op jit(solution)/shard_map/butterfly/pallas_call | solution.py:512
  52.7 2.6 %copy.10 = f32[2,262144]{1,0:T(2,128)} copy(f32[2,262144]{1,0:T(2,128)} %bitcast.8) | data formatting | bytes 4194304
where the time goes:
time: 56.3 us; the launch traced here: 55.3 us
  Pallas kernels  52.7 us (94%)
  local copies, waits for them, and re-layouts  2.61 us (5%)
    pallas_call x1, Pallas kernels, local(): pl.pallas_call(kernel, out_shape=jax.ShapeDtypeStruct((4096, 128), f32),...  52.7 us
    unnamed x1, local copies, waits for them, and re-layouts  2.61 us

commit v1 on v0

--- a/solution.py
+++ b/solution.py
@@ -16,6 +16,7 @@
 HALF = BOX_TICKS // 2
 N_BLK = 4
 MESH = pl.DeviceIdType.MESH
+SPAN = 32000.0
 
 
 def node_offsets(box_cells):
@@ -177,7 +178,7 @@
     return y[:, :128], y[:, 128:]
 
 
-LAG = 2
+LAG = 4
 
 
 def leaf_sums(pos, amp, spin_re, spin_im, mom, half):
@@ -279,50 +280,66 @@
         for half in range(2):
             tiles = [roots[q, z * 8 + (c * 2 + half)] for c in range(4)]
             parts[half].append(swap_lane(swap_lane(tiles, 1, 1), 0, 0))
-    out = []
+    lhs, inverse = [[], []], []
     for half in range(2):
         sides = []
         for c in range(2):
             rows = []
             for q in range(N_BLK):
                 rows += parts[half][q][2 * c : 2 * c + 2]
-            x = jnp.concatenate(rows, axis=0)
+            sides.append(jnp.concatenate(rows, axis=0))
+        reach = [jnp.sum(jnp.abs(x), axis=0, keepdims=True) for x in sides]
+        reach = jnp.maximum(jnp.maximum(reach[0], reach[1]), 1e-30)
+        scale = SPAN / reach
+        inverse.append(jnp.broadcast_to(reach * (1.0 / SPAN), (8, 128)))
+        for c, x in enumerate(sides):
+            x = x * scale
             hi = x.astype(jnp.bfloat16).astype(jnp.float32)
             t = jnp.concatenate([hi, x - hi], axis=0).T.astype(jnp.bfloat16)
-            sides.append(jnp.concatenate([t, t], axis=1))
-        out.append(sides)
-    return out
-
-
-def look_up(dense, tick, out, z, half, reverse):
+            lhs[c].append(jnp.concatenate([t, t], axis=1))
+    inverse = jnp.concatenate([jnp.concatenate(inverse, axis=1), jnp.zeros((120, 256), jnp.float32)], axis=0)
+    columns = jnp.concatenate([inverse[:, :128].T, inverse[:, 128:].T], axis=0)
+    return jnp.concatenate(lhs[0] + lhs[1], axis=0), columns
+
+
+def fill_dense(lhs, wave, dense):
+    for n in range(6):
+        cols = slice(n * 256, n * 256 + 256)
+        sums = jnp.dot(lhs, wave[:, cols], preferred_element_type=jnp.float32)
+        sums = (sums + (32768.0 + 0.5)).astype(jnp.int32)
+        dense[:, cols] = (sums[:256] << 16) | sums[256:]
+
+
+def look_up(dense, columns, tick, out, z, reverse):
     sub = lax.broadcasted_iota(jnp.int32, (8, 128), 0)
-    for i in range(16):
+    for i in range(32):
         row = i * 8
-        base = z * 256 + (half * 128 + row)
+        base = z * 256 + row
         y = tick[pl.ds(base, 8), :] - ((base + sub) * 64 + reverse) * BOX_TICKS - HALF
         upper = y >= 0
         index = jnp.where(upper, y, -1 - y)
         low, high = index & 127, index >> 7
-        sums = [None] * 4
+        pairs = [None, None]
         for h in range(6):
             pick = high == h
-            for c in range(2):
-                for part in range(2):
-                    start = part * HALF + h * 128
-                    got = jnp.take_along_axis(dense[c, row : row + 8, start : start + 128], low, axis=1)
-                    k = c * 2 + part
-                    sums[k] = got if h == 0 else jnp.where(pick, got, sums[k])
-        re_even, re_odd, im_even, im_odd = sums
-        re_odd = jnp.where(upper, re_odd, -re_odd)
-        im_odd = jnp.where(upper, im_odd, -im_odd)
-        out[pl.ds(base * 2, 8, stride=2), :] = re_even - im_odd
-        out[pl.ds(base * 2 + 1, 8, stride=2), :] = im_even + re_odd
+            for part in range(2):
+                start = part * HALF + h * 128
+                got = jnp.take_along_axis(dense[row : row + 8, start : start + 128], low, axis=1)
+                pairs[part] = got if h == 0 else jnp.where(pick, got, pairs[part])
+        even, odd = pairs
+        re_even, im_even = lax.shift_right_logical(even, 16) - 32768, (even & 65535) - 32768
+        re_odd, im_odd = lax.shift_right_logical(odd, 16) - 32768, (odd & 65535) - 32768
+        unit = jnp.broadcast_to(columns[row : row + 8, 0:1], (8, 128))
+        re = jnp.where(upper, re_even - im_odd, re_even + im_odd)
+        im = jnp.where(upper, im_even + re_odd, im_even - re_odd)
+        out[pl.ds(base * 2, 8, stride=2), :] = re.astype(jnp.float32) * unit
+        out[pl.ds(base * 2 + 1, 8, stride=2), :] = im.astype(jnp.float32) * unit
 
 
 def kernel(
     pos_in, amp_in, tick_in, stage_in, wave_in, shift_in, spin_in, out_hbm,
     pos, amp, tick, stage, wave, shift, spin, mom,
-    first_src, first_dst, second_src, roots, out, dense0, dense1,
+    first_src, first_dst, second_src, roots, out, dense,
     load_sem, store_sem, send1, recv1, send2, recv2, send3, recv3,
 ):
     leaf, blk = lax.axis_index("leaf"), lax.axis_index("blk")
@@ -339,7 +356,7 @@
         pltpu.make_async_copy(wave_in, wave, load_sem.at[7]),
         pltpu.make_async_copy(tick_in, tick, load_sem.at[8]),
     ]
-    for load in loads:
+    for load in loads[:3]:
         load.start()
     barrier = pltpu.get_barrier_semaphore()
 
@@ -351,8 +368,12 @@
     for i in range(1, N_BLK):
         pl.semaphore_signal(barrier, inc=1, device_id={"blk": (blk + i) % N_BLK}, device_id_type=MESH)
 
+    for load in loads[3:5]:
+        load.start()
     for load in loads[:3]:
         load.wait()
+    for load in loads[5:]:
+        load.start()
     spin_re, spin_im = spin[0], spin[1]
     leaf_sums(pos, amp, spin_re, spin_im, mom, 0)
     for load in loads[3:5]:
@@ -372,15 +393,27 @@
             device_id_type=MESH,
         )
 
-    def first_send(i, carry):
-        first(i).start()
+    def far_first(n):
+        k = n // 8
+        step = (k + 1) // 2
+        off = (4 + step * (1 - 2 * (k % 2)) + 8) % 8
+        z = (own_z + off) % 8
+        return (z * 8 + n % 8) ^ leaf
+
+    def first_send(n, carry):
+        i = far_first(n)
+
+        @pl.when(i != 0)
+        def _():
+            first(i).start()
+
         return carry
 
     def first_wait(i, carry):
         first(i).wait()
         return carry
 
-    lax.fori_loop(1, 64, first_send, 0)
+    lax.fori_loop(0, 64, first_send, 0)
     first_dst[leaf] = first_src[leaf]
     loads[6].wait()
     lax.fori_loop(1, 64, first_wait, 0)
@@ -477,12 +510,9 @@
             z = near_z(c - LAG)
             for i in (1, 2, 3):
                 third_got(z, i).wait_recv()
-            lhs = coefficients(roots, z)
-            for half, dense in enumerate((dense0, dense1)):
-                for side in range(2):
-                    dense[side] = jnp.dot(lhs[half][side], wave[...], preferred_element_type=jnp.float32)
-            for half, dense in enumerate((dense0, dense1)):
-                look_up(dense, tick, out, z, half, reverse)
+            lhs, columns = coefficients(roots, z)
+            fill_dense(lhs, wave, dense)
+            look_up(dense, columns, tick, out, z, reverse)
             store(z).start()
 
         return carry
@@ -528,8 +558,7 @@
             vmem(tiles, f32),
             vmem((N_BLK, *tiles), f32),
             vmem((4096, 128), f32),
-            vmem((2, 128, 2 * HALF), f32),
-            vmem((2, 128, 2 * HALF), f32),
+            vmem((256, 2 * HALF), jnp.int32),
             dma((9,)),
             dma((8,)),
             dma((64,)),

time: 56.3 us -> 52.3 us (0.929); the launches traced: 55.3 us -> 52.2 us
  Pallas kernels: 52.7 us -> 49.6 us
    pallas_call x1, Pallas kernels: 52.7 us -> 49.6 us  [local(): pl.pallas_call(kernel, out_shape=jax.ShapeDtypeStruct((4096, 128), f32),...]
where the time goes in v1:
time: 52.3 us; the launch traced here: 52.2 us
  Pallas kernels  49.6 us (95%)
  local copies, waits for them, and re-layouts  2.61 us (5%)
    pallas_call x1, Pallas kernels, local(): pl.pallas_call(kernel, out_shape=jax.ShapeDtypeStruct((4096, 128), f32),...  49.6 us
    unnamed x1, local copies, waits for them, and re-layouts  2.61 us

profile of v1, /device:TPU:1, one launch (start us, length us, event | category | flops | bytes accessed | tf_op | source)
XLA Modules:
  0.0 52.2 jit_solution(6231694579055751698)
XLA Ops:
  0.0 49.6 %butterfly.1 = f32[4096,128]{1,0:T(8,128)} custom-call(s32[4,2,256,128]{3,2,1,0:T(8,128)} %bitcast.10, f32[2,4,2,256,128]{4,3,2,1,0:T(8,128)} %bitcast.9, s32[2048,128]{1,0:T(8,128)} %bitcast.11, bf16[6,2,256,256]{3,2,1,0:T(8,128)(2,1)} %constant.8.clone.stage_in, bf16[256,1536]{1,0:T(8,128)(2,1)} %constant.9.clone.wave_in, ...), custom_call_target="tpu_custom_call" | custom-call | tf_op jit(solution)/shard_map/butterfly/pallas_call | solution.py:542
  49.6 2.6 %copy.10 = f32[2,262144]{1,0:T(2,128)} copy(f32[2,262144]{1,0:T(2,128)} %bitcast.8) | data formatting | bytes 4194304

commit v2 on v1

--- a/solution.py
+++ b/solution.py
@@ -337,10 +337,10 @@
 
 
 def kernel(
-    pos_in, amp_in, tick_in, stage_in, wave_in, shift_in, spin_in, out_hbm,
+    pos_in, amp_in, tick_in, stage_in, wave_in, shift_in, spin_in, out,
     pos, amp, tick, stage, wave, shift, spin, mom,
-    first_src, first_dst, second_src, roots, out, dense,
-    load_sem, store_sem, send1, recv1, send2, recv2, send3, recv3,
+    first_src, first_dst, second_src, roots, dense,
+    load_sem, send1, recv1, send2, recv2, send3, recv3,
 ):
     leaf, blk = lax.axis_index("leaf"), lax.axis_index("blk")
     own_z = leaf // 8
@@ -483,11 +483,6 @@
             device_id_type=MESH,
         )
 
-    def store(z):
-        return pltpu.make_async_copy(
-            out.at[pl.ds(z * 512, 512)], out_hbm.at[pl.ds(z * 512, 512)], store_sem.at[z]
-        )
-
     reverse = jnp.int32(0)
     for bit in range(6):
         reverse = reverse * 2 + (leaf // 2**bit) % 2
@@ -513,14 +508,12 @@
             lhs, columns = coefficients(roots, z)
             fill_dense(lhs, wave, dense)
             look_up(dense, columns, tick, out, z, reverse)
-            store(z).start()
 
         return carry
 
     lax.fori_loop(0, 8 + LAG, chunk_step, 0)
 
     def finish(z, carry):
-        store(z).wait()
         for i in (1, 2, 3):
             third(z, i).wait_send()
         return carry
@@ -541,9 +534,9 @@
     f32, tiles = jnp.float32, (64, 8, 128)
     out = pl.pallas_call(
         kernel,
-        out_shape=jax.ShapeDtypeStruct((4096, 128), f32),
+        out_shape=pltpu.VMEM((4096, 128), f32),
         in_specs=[hbm] * 7,
-        out_specs=hbm,
+        out_specs=pl.BlockSpec(memory_space=pltpu.VMEM),
         scratch_shapes=[
             vmem((4, 2, 256, 128), jnp.int32),
             vmem((2, 4, 2, 256, 128), f32),
@@ -557,10 +550,8 @@
             vmem(tiles, f32),
             vmem(tiles, f32),
             vmem((N_BLK, *tiles), f32),
-            vmem((4096, 128), f32),
             vmem((256, 2 * HALF), jnp.int32),
             dma((9,)),
-            dma((8,)),
             dma((64,)),
             dma((64,)),
             dma((64,)),

time: 52.3 us -> 50.3 us (0.962)
  local copies, waits for them, and re-layouts: 2.61 us -> 1.32 us
  Pallas kernels: 49.6 us -> 48.9 us
    unnamed x1, local copies, waits for them, and re-layouts: 2.61 us -> 1.32 us
    pallas_call x1, Pallas kernels: 49.6 us -> 48.9 us  [local(): pl.pallas_call(kernel, out_shape=pltpu.VMEM((4096, 128), f32), in_specs=[...]
where the time goes in v2:
time: 50.3 us; the launch traced here: 50.2 us
  Pallas kernels  48.9 us (97%)
  local copies, waits for them, and re-layouts  1.32 us (3%)
    pallas_call x1, Pallas kernels, local(): pl.pallas_call(kernel, out_shape=pltpu.VMEM((4096, 128), f32), in_specs=[...  48.9 us
    unnamed x1, local copies, waits for them, and re-layouts  1.32 us

profile of v2, /device:TPU:1, one launch (start us, length us, event | category | flops | bytes accessed | tf_op | source)
XLA Modules:
  0.0 50.2 jit_solution(4000352749785862863)
XLA Ops:
  0.0 48.9 %butterfly.1 = f32[4096,128]{1,0:T(8,128)S(1)} custom-call(s32[4,2,256,128]{3,2,1,0:T(8,128)} %bitcast.10, f32[2,4,2,256,128]{4,3,2,1,0:T(8,128)} %bitcast.9, s32[2048,128]{1,0:T(8,128)} %bitcast.11, bf16[6,2,256,256]{3,2,1,0:T(8,128)(2,1)} %constant.8.clone.stage_in, bf16[256,1536]{1,0:T(8,128)(2,1)} %constant.9.clone.wave_in, ...), custom_call_target="tpu_custom_call" | custom-call | tf_op jit(solution)/shard_map/butterfly/pallas_call | solution.py:535
  48.9 1.3 %copy.10 = f32[2,262144]{1,0:T(2,128)} copy(f32[2,262144]{1,0:T(2,128)S(1)} %bitcast.8) | data formatting | bytes 4194304
